TPU v7x, 32 devices: a whole 2x2x4 slice. The times are simulated.
32 devices in a mesh: groups: 2 (over y), gx: 16 (over z, x, core).
Axes of the slice: x: 2, y: 2, z: 4, core: 2. Of those that a mesh axis runs over, the one named last changes fastest.
Arguments:
- pressure: float32 [7, 256, 128, 128], P(None, ('groups', 'gx')), parts along dimension 1, may hold values from -6 to 6
- adjoint: float32 [7, 256, 128, 128], P(None, ('groups', 'gx')), parts along dimension 1, may hold values from -6 to 6
- permeability: float32 [3, 256, 128, 128], P(None, ('groups', 'gx')), parts along dimension 1, may hold values from 0.02 to 40, as said below
- active: int32 [256, 128, 128], P(('groups', 'gx')), parts along dimension 0, may hold values 0 or 1
- fault_codes: int32 [3, 256, 128, 128], P(None, ('groups', 'gx')), parts along dimension 1, may hold values from 0 to 3
Outputs:
- gradient: float32 [3, 256, 128, 128], P(None, ('groups', 'gx')), parts along dimension 1
There are 2 independent parts, one for each index of `groups`. A program takes and returns all parts, laid end to end along the dimension named above; each array names one. Nothing has to cross between parts.
Inputs may be any that keep to these rules, and one draw needn't show every extreme that they name: `permeability`: Positive.
All inputs are finite; a program needn't handle non-finite values. No bound on the sum of `active` on one device may be relied on, other than what follows from the above.
Results may differ from a plain program's by a relative error of at most 0.0003.
Values sent between devices are 32-bit elements; how exact they have to be, the bound alone decides.
A program may use at most 64 MiB of HBM per device.

v0:
```python
import jax
import jax.numpy as jnp
from jax import lax
from jax.sharding import PartitionSpec as P

epsilon = 1e-06


def shifted(value, axis, by):
    count = lax.axis_size(axis)
    pairs = [(i, i + by) for i in range(count) if 0 <= i + by < count]
    return lax.ppermute(value, axis, pairs)


def multiplier(codes):
    return jnp.where(
        codes == 0, 1.0, jnp.where(codes == 1, 0.6, jnp.where(codes == 2, 0.25, 0.05))
    ).astype(jnp.float32)


def pair_terms(lower_pres, upper_pres, lower_adj, upper_adj, lower_perm, upper_perm, factor):
    products = jnp.sum((lower_adj - upper_adj) * (lower_pres - upper_pres), axis=0)
    summed = lower_perm + upper_perm
    scaled = 2.0 * factor * products / (summed * summed)
    return (scaled * upper_perm * upper_perm, scaled * lower_perm * lower_perm)


def cut(values, start, stop, along):
    return lax.slice_in_dim(values, start, stop, axis=along)


def direction_grad(pressure, adjoint, perm_dir, opened, codes, along):
    count = opened.shape[along]
    factor = (
        multiplier(cut(codes, 0, count - 1, along))
        * cut(opened, 0, count - 1, along)
        * cut(opened, 1, count, along)
    )
    to_lower, to_upper = pair_terms(
        cut(pressure, 0, count - 1, along + 1),
        cut(pressure, 1, count, along + 1),
        cut(adjoint, 0, count - 1, along + 1),
        cut(adjoint, 1, count, along + 1),
        cut(perm_dir, 0, count - 1, along),
        cut(perm_dir, 1, count, along),
        factor,
    )
    widths_lower = [(0, 0), (0, 0), (0, 0)]
    widths_upper = [(0, 0), (0, 0), (0, 0)]
    widths_lower[along] = (0, 1)
    widths_upper[along] = (1, 0)
    return jnp.pad(to_lower, widths_lower) + jnp.pad(to_upper, widths_upper)


def local(pressure, adjoint, permeability, active, fault_codes):
    opened = active.astype(jnp.float32)
    layers = opened.shape[0]
    steps = pressure.shape[0]
    perm_first = permeability[0]
    grad_first = direction_grad(pressure, adjoint, perm_first, opened, fault_codes[0], 0)
    grad_second = direction_grad(pressure, adjoint, permeability[1], opened, fault_codes[1], 1)
    grad_third = direction_grad(pressure, adjoint, permeability[2], opened, fault_codes[2], 2)
    last = layers - 1
    mult_last = multiplier(fault_codes[0, last])
    lowest = jnp.concatenate([pressure[:, 0], adjoint[:, 0], perm_first[0:1], opened[0:1]], axis=0)
    above = shifted(lowest, "gx", -1)
    to_lower, outgoing = pair_terms(
        pressure[:, last],
        above[:steps],
        adjoint[:, last],
        above[steps : 2 * steps],
        perm_first[last],
        above[2 * steps],
        mult_last * opened[last] * above[2 * steps + 1],
    )
    to_upper = shifted(outgoing, "gx", 1)
    grad_first = grad_first.at[last].add(to_lower)
    grad_first = grad_first.at[0].add(to_upper)
    stacked = jnp.stack(
        [perm_first * grad_first, permeability[1] * grad_second, permeability[2] * grad_third]
    )
    local_sum = jnp.sum(stacked * stacked)
    total = lax.psum(local_sum, "gx")
    entries = 3 * layers * lax.axis_size("gx") * opened.shape[1] * opened.shape[2]
    root_mean = jnp.sqrt(total / entries + epsilon)
    return stacked / root_mean


def solution(mesh):
    placed = (
        P(None, ("groups", "gx"), None, None),
        P(None, ("groups", "gx"), None, None),
        P(None, ("groups", "gx"), None, None),
        P(("groups", "gx"), None, None),
        P(None, ("groups", "gx"), None, None),
    )
    return jax.shard_map(
        local,
        mesh=mesh,
        in_specs=placed,
        out_specs=P(None, ("groups", "gx"), None, None),
        check_vma=False,
    )
```

profile of v0, /device:TPU:0, one launch (start us, length us, event | category | flops | bytes accessed | tf_op | source)
XLA Modules:
  0.0 60.2 jit_solution(11112736705899498444)
XLA Ops:
  0.0 0.0 copy-start
  0.0 1.2 %convert_element_type.15 = f32[8,128,128]{2,1,0:T(8,128)S(1)} convert(s32[8,128,128]{2,1,0:T(8,128)} %param.12) | non-fusion elementwise | flops 131072 | bytes 1048576 | tf_op jit(solution)/shard_map/convert_element_type | solution.py:56
  1.3 0.9 %slice_bitcast_fusion.6 = f32[1,128,128]{2,1,0:T(8,128)S(1)} fusion(f32[3,8,128,128]{3,2,1,0:T(8,128)} %param.11), kind=kLoop, calls=%fused_computation.68 | loop fusion | bytes 131072 | tf_op jit(solution)/shard_map/slice | solution.py:65
  2.1 1.2 %slice_bitcast_fusion.4 = (f32[7,128,128]{2,1,0:T(8,128)S(1)}, f32[7,128,128]{2,1,0:T(8,128)S(1)}) fusion(f32[7,8,128,128]{3,2,1,0:T(8,128)} %param.10, f32[7,8,128,128]{3,2,1,0:T(8,128)} %param.9), kind=kLoop, calls=%fused_computation.45 | loop fusion | bytes 1835008 | tf_op jit(solution)/shard_map/squeeze | solution.py:65
  3.3 0.1 pad_maximum_fusion.1
  3.4 0.0 copy-start.2
  3.4 1.4 %collective-permute-start = (f32[16,128,128]{2,1,0:T(8,128)S(1)}, f32[16,128,128]{2,1,0:T(8,128)S(1)}, u32[]{:S(2)}, u32[]{:S(2)}) collective-permute-start(f32[16,128,128]{2,1,0:T(8,128)S(1)} %pad_maximum_fusion.1), channel_id=1, source_target_pairs={{1,0},{2,1},{3,2},{4,3},{5,4},{6,5},{7,6},{8,7},{9,8},{10,9},{11,1... | collective-permute-start | bytes 3145736 | tf_op jit(solution)/shard_map/ppermute | solution.py:12
  4.9 0.0 copy-done
  4.9 0.0 copy-start.1
  4.9 4.2 %multiply_reduce_fusion.2 = f32[7,128,128]{2,1,0:T(8,128)S(1)} fusion(f32[7,8,128,128]{3,2,1,0:T(8,128)S(1)} %copy-done, f32[7,8,128,128]{3,2,1,0:T(8,128)} %param.10), kind=kLoop, calls=%fused_computation.2 | loop fusion | flops 3096576 | bytes 13303808 | tf_op jit(solution)/shard_map/reduce_sum | solution.py:22
  9.1 0.0 copy-done.2
  9.1 0.1 slice_bitcast_fusion.3
  9.2 0.0 copy-done.1
  9.2 0.0 copy-start.3
  9.2 2.0 %multiply_reduce_fusion = f32[8,128,127]{2,1,0:T(8,128)S(1)} fusion(f32[7,8,128,128]{3,2,1,0:T(8,128)S(1)} %copy-done, f32[7,8,128,128]{3,2,1,0:T(8,128)S(1)} %copy-done.1), kind=kLoop, calls=%fused_computation | loop fusion | flops 3511296 | bytes 15085568 | tf_op jit(solution)/shard_map/reduce_sum | solution.py:22
  11.2 0.0 copy-done.3
  11.2 0.1 slice_bitcast_fusion.2
  11.3 0.2 multiply_multiply_fusion.5
  11.6 0.1 multiply_multiply_fusion.4
  11.6 0.4 multiply_multiply_fusion.1
  12.0 0.1 multiply_multiply_fusion
  12.1 0.1 pad_add_fusion
  12.1 1.8 %multiply_reduce_fusion.1 = f32[8,127,128]{2,1,0:T(8,128)S(1)} fusion(f32[7,8,128,128]{3,2,1,0:T(8,128)S(1)} %copy-done, f32[7,8,128,128]{3,2,1,0:T(8,128)S(1)} %copy-done.1), kind=kLoop, calls=%fused_computation.1 | loop fusion | flops 3511296 | bytes 15085568 | tf_op jit(solution)/shard_map/reduce_sum | solution.py:22
  14.0 0.3 multiply_multiply_fusion.3
  14.3 0.1 multiply_multiply_fusion.2
  14.4 0.0 collective-permute-done
  14.4 0.1 fusion.9
  14.6 8.5 %collective-permute-start.1 = (f32[128,128]{1,0:T(8,128)S(1)}, f32[128,128]{1,0:T(8,128)S(1)}, u32[]{:S(2)}, u32[]{:S(2)}) collective-permute-start(f32[128,128]{1,0:T(8,128)S(1)} %multiply_multiply_fusion.6), channel_id=1, source_target_pairs={{0,1},{1,2},{2,3},{3,4},{4,5},{5,6},{6,7},{7,8},{8,9},{9,10},{10,1... | collective-permute-start | bytes 196616 | tf_op jit(solution)/shard_map/ppermute | solution.py:12
  23.2 0.8 %collective-permute-done.1 = f32[128,128]{1,0:T(8,128)S(1)} collective-permute-done((f32[128,128]{1,0:T(8,128)S(1)}, f32[128,128]{1,0:T(8,128)S(1)}, u32[]{:S(2)}, u32[]{:S(2)}) %collective-permute-start.1) | collective-permute-done | bytes 65568 | tf_op jit(solution)/shard_map/ppermute | solution.py:12
  24.0 0.4 fusion.7
  24.4 1.0 %multiply_reduce_fusion.3 = f32[]{:T(128)} fusion(f32[1,8,128,128]{3,2,1,0:T(8,128)S(1)} %get-tuple-element.37, f32[1,8,128,128]{3,2,1,0:T(8,128)S(1)} %get-tuple-element.36, f32[1,8,128,128]{3,2,1,0:T(8,128)S(1)} %get-tuple-element.35), kind=kLoop, calls=%fused_computation.4 | loop fusion | flops 1572863 | bytes 1572868 | tf_op jit(solution)/shard_map/reduce_sum | solution.py:82
  25.4 32.8 %psum.7 = f32[]{:T(128)} all-reduce(f32[]{:T(128)} %multiply_reduce_fusion.3), channel_id=1, replica_groups=mesh['groups'=2,'gx'=16] {'gx'}, use_global_device_ids=true, to_apply=%region_5.6 | all-reduce | flops 1 | bytes 8 | tf_op jit(solution)/shard_map/psum | solution.py:83
  58.9 1.3 %fusion = f32[3,8,128,128]{3,2,1,0:T(8,128)} fusion(f32[1,8,128,128]{3,2,1,0:T(8,128)S(1)} %get-tuple-element.37, f32[1,8,128,128]{3,2,1,0:T(8,128)S(1)} %get-tuple-element.36, f32[1,8,128,128]{3,2,1,0:T(8,128)S(1)} %get-tuple-element.35, f32[]{:T(128)S(6)} %sqrt.3), kind=kLoop, calls=%fused_computation.5 | loop fusion | flops 1179648 | bytes 3145732 | tf_op jit(solution)/shard_map/div | solution.py:86
  (4 shorter events, 0.1 us)
Async XLA Ops:
  0.0 4.9 %copy-start = (f32[7,8,128,128]{3,2,1,0:T(8,128)S(1)}, f32[7,8,128,128]{3,2,1,0:T(8,128)}, u32[]{:S(2)}) copy-start(f32[7,8,128,128]{3,2,1,0:T(8,128)} %param.9) | copy-start | bytes 11010052
  3.4 5.7 %copy-start.2 = (f32[3,8,128,128]{3,2,1,0:T(8,128)S(1)}, f32[3,8,128,128]{3,2,1,0:T(8,128)}, u32[]{:S(2)}) copy-start(f32[3,8,128,128]{3,2,1,0:T(8,128)} %param.11) | copy-start | bytes 4718596
  3.4 11.0 %collective-permute-start = (f32[16,128,128]{2,1,0:T(8,128)S(1)}, f32[16,128,128]{2,1,0:T(8,128)S(1)}, u32[]{:S(2)}, u32[]{:S(2)}) collective-permute-start(f32[16,128,128]{2,1,0:T(8,128)S(1)} %pad_maximum_fusion.1), channel_id=1, source_target_pairs={{1,0},{2,1},{3,2},{4,3},{5,4},{6,5},{7,6},{8,7},{9,8},{10,9},{11,1... | collective-permute-start | bytes 3145736 | tf_op jit(solution)/shard_map/ppermute | solution.py:12
  4.9 4.3 %copy-start.1 = (f32[7,8,128,128]{3,2,1,0:T(8,128)S(1)}, f32[7,8,128,128]{3,2,1,0:T(8,128)}, u32[]{:S(2)}) copy-start(f32[7,8,128,128]{3,2,1,0:T(8,128)} %param.10) | copy-start | bytes 11010052
  9.2 2.0 %copy-start.3 = (s32[3,8,128,128]{3,2,1,0:T(8,128)S(1)}, s32[3,8,128,128]{3,2,1,0:T(8,128)}, u32[]{:S(2)}) copy-start(s32[3,8,128,128]{3,2,1,0:T(8,128)} %param.13) | copy-start | bytes 4718596
  14.6 9.4 %collective-permute-start.1 = (f32[128,128]{1,0:T(8,128)S(1)}, f32[128,128]{1,0:T(8,128)S(1)}, u32[]{:S(2)}, u32[]{:S(2)}) collective-permute-start(f32[128,128]{1,0:T(8,128)S(1)} %multiply_multiply_fusion.6), channel_id=1, source_target_pairs={{0,1},{1,2},{2,3},{3,4},{4,5},{5,6},{6,7},{7,8},{8,9},{9,10},{10,1... | collective-permute-start | bytes 196616 | tf_op jit(solution)/shard_map/ppermute | solution.py:12
where the time goes:
time: 60.4 us; the launch traced here: 60.2 us
  blocking collectives  32.8 us (54%)
  other arithmetic  13.4 us (22%)
  starting transfers between devices  9.95 us (16%)
  local copies, waits for them, and re-layouts  2.28 us (4%)
  between operations  0.91 us (2%)
  waiting for transfers between devices  0.83 us (1%)
    psum x1, blocking collectives, local(): total = lax.psum(local_sum, 'gx')  32.8 us
    ppermute x2, starting transfers between devices, shifted(): return lax.ppermute(value, axis, pairs)  9.95 us
    reduce_sum x4, other arithmetic, pair_terms(): jnp.sum((lower_adj - upper_adj) * (lower_pres - upper_pres), axis=0)  8.1 us
    div x1, other arithmetic, local(): return stacked / root_mean  1.33 us
    convert_element_type x1, other arithmetic, local(): opened = active.astype(jnp.float32)  1.23 us
    squeeze x1, local copies, waits for them, and re-layouts, local(): adjoint[:, 0]  1.22 us
  transfers between devices with their start and end apart: 2, of which 1 were waited for; matrix products, arithmetic and copies ran while one was open for 16% of the time, Pallas kernels for 0%

commit v1 on v0

v1 whole, which is shorter than its diff:
```python
import functools

import jax
import jax.numpy as jnp
from jax import lax
from jax.experimental import pallas as pl
from jax.experimental.pallas import tpu as pltpu
from jax.sharding import PartitionSpec as P

MESH = pl.DeviceIdType.MESH
epsilon = 1e-06
ROWS = 32
PAD = 8


def multiplier(codes):
    return jnp.where(codes == 0, 1.0, jnp.where(codes == 1, 0.6, jnp.where(codes == 2, 0.25, 0.05))).astype(jnp.float32)


def fold(values):
    squares = values * values
    total = squares[0:8]
    for i in range(8, squares.shape[0], 8):
        total = total + squares[i : i + 8]
    return total


def weight(products, factor, k_lo, k_up):
    summed = k_lo + k_up
    return 2.0 * factor * products * (k_lo * k_up) / (summed * summed)


def kernel(
    n, entries, p_hbm, a_hbm, k_hbm, act_hbm, code_hbm, grad, scale,
    p, a, k, act, code, halo_p, halo_a, halo_g, g_out, ret_out, ret_in, tail, part, parts,
    load_sem, halo_send, halo_recv, ret_send, ret_recv, part_send, part_recv,
):
    me = lax.axis_index("gx")
    lower, upper = me - 1, me + 1
    steps, layers, height, width = p_hbm.shape
    last = layers - 1
    blocks = height // ROWS

    barrier = pltpu.get_barrier_semaphore()

    def greet(j, carry):
        pl.semaphore_signal(barrier, inc=1, device_id={"gx": lax.rem(me + j, n)}, device_id_type=MESH)
        return carry

    lax.fori_loop(1, n, greet, 0)

    def loads(l):
        return (
            pltpu.make_async_copy(k_hbm.at[:, l], k.at[:, l, pl.ds(0, height)], load_sem.at[2, l]),
            pltpu.make_async_copy(act_hbm.at[l], act.at[l, pl.ds(0, height)], load_sem.at[3, l]),
            pltpu.make_async_copy(code_hbm.at[:, l], code.at[:, l], load_sem.at[4, l]),
            pltpu.make_async_copy(p_hbm.at[:, l], p.at[:, l, pl.ds(0, height)], load_sem.at[0, l]),
            pltpu.make_async_copy(a_hbm.at[:, l], a.at[:, l, pl.ds(0, height)], load_sem.at[1, l]),
        )

    def halo_pa(c):
        rows = pl.ds(c * ROWS, ROWS)
        return (
            pltpu.make_async_remote_copy(
                src_ref=p_hbm.at[:, 0, rows], dst_ref=halo_p.at[:, rows],
                send_sem=halo_send.at[2 * c], recv_sem=halo_recv.at[2 * c],
                device_id={"gx": lower}, device_id_type=MESH),
            pltpu.make_async_remote_copy(
                src_ref=a_hbm.at[:, 0, rows], dst_ref=halo_a.at[:, rows],
                send_sem=halo_send.at[2 * c + 1], recv_sem=halo_recv.at[2 * c + 1],
                device_id={"gx": lower}, device_id_type=MESH),
        )

    halo_k = pltpu.make_async_remote_copy(
        src_ref=g_out, dst_ref=halo_g, send_sem=halo_send.at[2 * blocks], recv_sem=halo_recv.at[2 * blocks],
        device_id={"gx": lower}, device_id_type=MESH)

    def returned(c):
        rows = pl.ds(c * ROWS, ROWS)
        return pltpu.make_async_remote_copy(
            src_ref=ret_out.at[rows], dst_ref=ret_in.at[rows], send_sem=ret_send.at[c], recv_sem=ret_recv.at[c],
            device_id={"gx": upper}, device_id_type=MESH)

    first = loads(0)
    for copy in first[:3]:
        copy.start()

    pl.semaphore_wait(barrier, n - 1)

    @pl.when(me > 0)
    def _():
        for copy in halo_pa(0):
            copy.start()

    for copy in first[3:]:
        copy.start()

    def start_layer(l, carry):
        for copy in loads(l):
            copy.start()
        return carry

    lax.fori_loop(1, layers, start_layer, 0)
    for copy in first[:2]:
        copy.wait()
    g_out[...] = k[0, 0, 0:height] * act[0, 0:height].astype(jnp.float32)

    @pl.when(me > 0)
    def _():
        halo_k.start()
        for c in range(1, blocks):
            for copy in halo_pa(c):
                copy.start()

    for copy in first[2:]:
        copy.wait()
    tail[0:8] = jnp.zeros((8, width), jnp.float32)
    lane = lax.broadcasted_iota(jnp.int32, (ROWS, width), 1)
    row = lax.broadcasted_iota(jnp.int32, (ROWS, width), 0)
    grad[0, 0] = jnp.zeros((height, width), jnp.float32)

    def layer(l, total):
        @pl.when(l < last)
        def _():
            for copy in loads(l + 1):
                copy.wait()

        def block(b, total):
            r = pl.multiple_of(b * ROWS, ROWS)
            here, after = pl.ds(r, ROWS), pl.ds(r + 1, ROWS)
            prod_y = jnp.zeros((ROWS, width), jnp.float32)
            prod_z = jnp.zeros((ROWS, width), jnp.float32)
            for t in range(steps):
                pt, at = p[t, l, here], a[t, l, here]
                prod_y += (at - a[t, l, after]) * (pt - p[t, l, after])
                prod_z += (at - pltpu.roll(at, width - 1, 1)) * (pt - pltpu.roll(pt, width - 1, 1))
            opened = act[l, here].astype(jnp.float32)
            k1 = k[1, l, here]
            k1_up = k[1, l, after]
            factor = multiplier(code[1, l, here]) * opened * act[l, after].astype(jnp.float32)
            w = jnp.where(row + r < height - 1, weight(prod_y, factor, k1, k1_up), 0.0)
            w_lo = jnp.where(row + r < height - 1, w * k1_up, 0.0)
            tail[pl.ds(r + 8, ROWS)] = w * k1
            log1 = w_lo + tail[pl.ds(r + 7, ROWS)]
            grad[1, l, here] = log1
            k2 = k[2, l, here]
            k2_up = pltpu.roll(k2, width - 1, 1)
            factor = multiplier(code[2, l, here]) * opened * pltpu.roll(opened, width - 1, 1)
            w = jnp.where(lane < width - 1, weight(prod_z, factor, k2, k2_up), 0.0)
            log2 = w * k2_up + pltpu.roll(w * k2, 1, 1)
            grad[2, l, here] = log2
            return total + fold(log1) + fold(log2)

        total = lax.fori_loop(0, blocks, block, total)

        def cross(b, total):
            here = pl.ds(pl.multiple_of(b * ROWS, ROWS), ROWS)
            prod = jnp.zeros((ROWS, width), jnp.float32)
            for t in range(steps):
                prod += (a[t, l, here] - a[t, l + 1, here]) * (p[t, l, here] - p[t, l + 1, here])
            k0, k0_up = k[0, l, here], k[0, l + 1, here]
            factor = multiplier(code[0, l, here]) * (act[l, here] * act[l + 1, here]).astype(jnp.float32)
            w = weight(prod, factor, k0, k0_up)
            log0 = grad[0, l, here] + w * k0_up
            grad[0, l, here] = log0
            grad[0, l + 1, here] = w * k0
            return total + jnp.where(l > 0, 1.0, 0.0) * fold(log0)

        return lax.cond(l < last, lambda total: lax.fori_loop(0, blocks, cross, total), lambda total: total, total)

    total = lax.fori_loop(0, layers, layer, jnp.zeros((8, width), jnp.float32))
    part[...] = total

    @pl.when(me < n - 1)
    def _():
        halo_k.wait_recv()
        for c in range(blocks):
            for copy in halo_pa(c):
                copy.wait_recv()
            here = pl.ds(c * ROWS, ROWS)
            prod = jnp.zeros((ROWS, width), jnp.float32)
            for t in range(steps):
                prod += (a[t, last, here] - halo_a[t, here]) * (p[t, last, here] - halo_p[t, here])
            k0, g_up = k[0, last, here], halo_g[here]
            factor = multiplier(code[0, last, here]) * act[last, here].astype(jnp.float32)
            w = weight(prod, factor, k0, g_up)
            ret_out[here] = w * k0
            returned(c).start()
            grad[0, last, here] = grad[0, last, here] + w * g_up

    part[...] = part[...] + fold(grad[0, last])

    @pl.when(me > 0)
    def _():
        for c in range(blocks):
            here = pl.ds(c * ROWS, ROWS)
            returned(c).wait_recv()
            grad[0, 0, here] = grad[0, 0, here] + ret_in[here]

    part[...] = part[...] + fold(grad[0, 0])

    def to_peer(j):
        return pltpu.make_async_remote_copy(
            src_ref=part, dst_ref=parts.at[j - 1], send_sem=part_send.at[j - 1], recv_sem=part_recv.at[j - 1],
            device_id={"gx": lax.rem(me + j, n)}, device_id_type=MESH)

    def send(j, carry):
        to_peer(j).start()
        return carry

    def receive(j, carry):
        to_peer(j).wait_recv()
        return carry

    lax.fori_loop(1, n, send, 0)
    lax.fori_loop(1, n, receive, 0)
    whole = jnp.sum(jnp.sum(parts[...], axis=0) + part[...], keepdims=True)
    scale[...] = jnp.broadcast_to(lax.rsqrt(whole / entries + epsilon), scale.shape)

    def drain(j, carry):
        to_peer(j).wait_send()
        return carry

    lax.fori_loop(1, n, drain, 0)

    @pl.when(me > 0)
    def _():
        halo_k.wait_send()
        for c in range(blocks):
            for copy in halo_pa(c):
                copy.wait_send()

    @pl.when(me < n - 1)
    def _():
        for c in range(blocks):
            returned(c).wait_send()


def local(pressure, adjoint, permeability, active, fault_codes):
    n = lax.axis_size("gx")
    steps, layers, height, width = pressure.shape
    blocks = height // ROWS
    entries = 3 * layers * n * height * width
    f32 = jnp.float32
    padded = height + PAD
    dma = pltpu.SemaphoreType.DMA
    grad, scale = pl.pallas_call(
        functools.partial(kernel, n, entries),
        out_shape=(
            jax.ShapeDtypeStruct((3, layers, height, width), f32),
            jax.ShapeDtypeStruct((8, width), f32),
        ),
        in_specs=[pl.BlockSpec(memory_space=pltpu.HBM)] * 5,
        out_specs=(pl.BlockSpec(memory_space=pltpu.VMEM), pl.BlockSpec(memory_space=pltpu.VMEM)),
        scratch_shapes=[
            pltpu.VMEM((steps, layers, padded, width), f32),
            pltpu.VMEM((steps, layers, padded, width), f32),
            pltpu.VMEM((3, layers, padded, width), f32),
            pltpu.VMEM((layers, padded, width), jnp.int32),
            pltpu.VMEM((3, layers, height, width), jnp.int32),
            pltpu.VMEM((steps, height, width), f32),
            pltpu.VMEM((steps, height, width), f32),
            pltpu.VMEM((height, width), f32),
            pltpu.VMEM((height, width), f32),
            pltpu.VMEM((height, width), f32),
            pltpu.VMEM((height, width), f32),
            pltpu.VMEM((padded, width), f32),
            pltpu.VMEM((8, width), f32),
            pltpu.VMEM((n - 1, 8, width), f32),
            dma((5, layers)),
            dma((2 * blocks + 1,)),
            dma((2 * blocks + 1,)),
            dma((blocks,)),
            dma((blocks,)),
            dma((n - 1,)),
            dma((n - 1,)),
        ],
        compiler_params=pltpu.CompilerParams(collective_id=0, has_side_effects=True, vmem_limit_bytes=40 * 1024 * 1024),
        cost_estimate=pl.CostEstimate(flops=100_000_000, bytes_accessed=12_000_000, transcendentals=0),
    )(pressure, adjoint, permeability, active, fault_codes)
    return grad * scale[0, 0]


def solution(mesh):
    split = ("groups", "gx")
    placed = (P(None, split), P(None, split), P(None, split), P(split), P(None, split))
    return jax.shard_map(local, mesh=mesh, in_specs=placed, out_specs=P(None, split), check_vma=False)
```

time: 60.4 us -> 36.4 us (0.60)
  blocking collectives: 32.8 us -> 0 us
  Pallas kernels: 0 us -> 25.8 us
  other arithmetic: 13.4 us -> 1.86 us
  starting transfers between devices: 9.95 us -> 0 us
  local copies, waits for them, and re-layouts: 2.28 us -> 8.44 us
  between operations: 0.91 us -> 0.01 us
  waiting for transfers between devices: 0.83 us -> 0 us
    psum x1 -> x0, blocking collectives: 32.8 us -> none  [local(): total = lax.psum(local_sum, 'gx')]
    pallas_call x0 -> x1, Pallas kernels: none -> 25.8 us  [local(): pl.pallas_call(functools.partial(kernel, n, entries), out_shape=(jax.Shap...]
    ppermute x2 -> x0, starting transfers between devices: 9.95 us -> none  [shifted(): return lax.ppermute(value, axis, pairs)]
    reduce_sum x5 -> x0, other arithmetic: 9.1 us -> none  [the longest x4 8.1 us: pair_terms(): jnp.sum((lower_adj - upper_adj) * (lower_pres - upper_pres), axis=0)]
    unnamed x8 -> x10, local copies, waits for them, and re-layouts: 0.02 us -> 7.93 us
    squeeze x3 -> x0, local copies, waits for them, and re-layouts: 1.4 us -> none  [the longest x1 1.22 us: local(): adjoint[:, 0]]
    div x1 -> x0, other arithmetic: 1.33 us -> none  [local(): return stacked / root_mean]
    convert_element_type x1 -> x0, other arithmetic: 1.23 us -> none  [local(): opened = active.astype(jnp.float32)]
  transfers between devices with their start and end apart: 2 -> 0, of which waited for: 1 -> 0; matrix products, arithmetic and copies ran while one was open for 16% -> 0% of each run, Pallas kernels for 0% -> 0%
where the time goes in v1:
time: 36.4 us; the launch traced here: 36.2 us
  Pallas kernels  25.8 us (71%)
  local copies, waits for them, and re-layouts  8.44 us (23%)
  other arithmetic  1.86 us (5%)
    pallas_call x1, Pallas kernels, local(): pl.pallas_call(functools.partial(kernel, n, entries), out_shape=(jax.Shap...  25.8 us
    unnamed x10, local copies, waits for them, and re-layouts  7.93 us
    mul x1, other arithmetic, local(): return grad * scale[0, 0]  1.86 us

profile of v1, /device:TPU:0, one launch (start us, length us, event | category | flops | bytes accessed | tf_op | source)
XLA Modules:
  0.0 36.2 jit_solution(18077356250554512224)
XLA Ops:
  0.0 0.0 copy-start
  0.0 2.0 %copy-done = f32[7,8,128,128]{3,2,1,0:T(8,128)S(1)} copy-done((f32[7,8,128,128]{3,2,1,0:T(8,128)S(1)}, f32[7,8,128,128]{3,2,1,0:T(8,128)}, u32[]{:S(2)}) %copy-start) | copy-done | bytes 3670040
  2.0 0.0 copy-start.1
  2.0 2.0 %copy-done.1 = f32[7,8,128,128]{3,2,1,0:T(8,128)S(1)} copy-done((f32[7,8,128,128]{3,2,1,0:T(8,128)S(1)}, f32[7,8,128,128]{3,2,1,0:T(8,128)}, u32[]{:S(2)}) %copy-start.1) | copy-done | bytes 3670040
  4.1 0.0 copy-start.2
  4.1 1.4 %copy-done.2 = f32[3,8,128,128]{3,2,1,0:T(8,128)S(1)} copy-done((f32[3,8,128,128]{3,2,1,0:T(8,128)S(1)}, f32[3,8,128,128]{3,2,1,0:T(8,128)}, u32[]{:S(2)}) %copy-start.2) | copy-done | bytes 1572888
  5.5 0.0 copy-start.3
  5.5 1.4 %copy-done.3 = s32[3,8,128,128]{3,2,1,0:T(8,128)S(1)} copy-done((s32[3,8,128,128]{3,2,1,0:T(8,128)S(1)}, s32[3,8,128,128]{3,2,1,0:T(8,128)}, u32[]{:S(2)}) %copy-start.3) | copy-done | bytes 1572888
  6.9 0.0 copy-start.4
  6.9 1.0 %copy-done.4 = s32[8,128,128]{2,1,0:T(8,128)S(1)} copy-done((s32[8,128,128]{2,1,0:T(8,128)S(1)}, s32[8,128,128]{2,1,0:T(8,128)}, u32[]{:S(2)}) %copy-start.4) | copy-done | bytes 524312
  7.9 25.8 %shard_map.55 = (f32[3,8,128,128]{3,2,1,0:T(8,128)S(1)}, f32[8,128]{1,0:T(8,128)S(1)}) custom-call(f32[7,8,128,128]{3,2,1,0:T(8,128)S(1)} %copy-done, f32[7,8,128,128]{3,2,1,0:T(8,128)S(1)} %copy-done.1, f32[3,8,128,128]{3,2,1,0:T(8,128)S(1)} %copy-done.2, s32[8,128,128]{2,1,0:T(8,128)S(1)} %copy-done.4, s32[3,8,128,128]{3,2,1,0:T(8,128)S(1)} %copy-done.3), custom_call_target="tpu_custom_call" | custom-call | flops 100000000 | bytes 12000000 | tf_op jit(solution)/shard_map/pallas_call | solution.py:247
  33.8 0.5 %slice.3 = f32[1,1]{1,0:T(1,128)} slice(f32[8,128]{1,0:T(8,128)S(1)} %get-tuple-element.8), slice={[0:1], [0:1]} | slice | bytes 8 | tf_op jit(solution)/shard_map/slice | solution.py:281
  34.3 1.9 %broadcast_multiply_fusion = f32[3,8,128,128]{3,2,1,0:T(8,128)} fusion(f32[3,8,128,128]{3,2,1,0:T(8,128)S(1)} %get-tuple-element.7, f32[]{:T(128)} %bitcast), kind=kLoop, calls=%fused_computation | loop fusion | flops 393216 | bytes 3145732 | tf_op jit(solution)/shard_map/mul | solution.py:281
Async XLA Ops:
  0.0 2.0 %copy-start = (f32[7,8,128,128]{3,2,1,0:T(8,128)S(1)}, f32[7,8,128,128]{3,2,1,0:T(8,128)}, u32[]{:S(2)}) copy-start(f32[7,8,128,128]{3,2,1,0:T(8,128)} %p_hbm.1) | copy-start | bytes 11010052
  2.0 2.0 %copy-start.1 = (f32[7,8,128,128]{3,2,1,0:T(8,128)S(1)}, f32[7,8,128,128]{3,2,1,0:T(8,128)}, u32[]{:S(2)}) copy-start(f32[7,8,128,128]{3,2,1,0:T(8,128)} %a_hbm.1) | copy-start | bytes 11010052
  4.1 1.4 %copy-start.2 = (f32[3,8,128,128]{3,2,1,0:T(8,128)S(1)}, f32[3,8,128,128]{3,2,1,0:T(8,128)}, u32[]{:S(2)}) copy-start(f32[3,8,128,128]{3,2,1,0:T(8,128)} %k_hbm.1) | copy-start | bytes 4718596
  5.5 1.4 %copy-start.3 = (s32[3,8,128,128]{3,2,1,0:T(8,128)S(1)}, s32[3,8,128,128]{3,2,1,0:T(8,128)}, u32[]{:S(2)}) copy-start(s32[3,8,128,128]{3,2,1,0:T(8,128)} %code_hbm.1) | copy-start | bytes 4718596
  6.9 1.0 %copy-start.4 = (s32[8,128,128]{2,1,0:T(8,128)S(1)}, s32[8,128,128]{2,1,0:T(8,128)}, u32[]{:S(2)}) copy-start(s32[8,128,128]{2,1,0:T(8,128)} %act_hbm.1) | copy-start | bytes 1572868

commit v2 on v1

--- a/solution.py
+++ b/solution.py
@@ -31,9 +31,9 @@
 
 
 def kernel(
-    n, entries, p_hbm, a_hbm, k_hbm, act_hbm, code_hbm, grad, scale,
-    p, a, k, act, code, halo_p, halo_a, halo_g, g_out, ret_out, ret_in, tail, part, parts,
-    load_sem, halo_send, halo_recv, ret_send, ret_recv, part_send, part_recv,
+    n, entries, p_hbm, a_hbm, k_hbm, act_hbm, code_hbm, out_hbm, scale,
+    p, a, k, act, code, grad, halo_p, halo_a, halo_g, halo_own, g_out, ret_out, ret_in, tail, part, parts,
+    load_sem, out_sem, halo_send, halo_recv, ret_send, ret_recv, part_send, part_recv,
 ):
     me = lax.axis_index("gx")
     lower, upper = me - 1, me + 1
@@ -75,6 +75,13 @@
         src_ref=g_out, dst_ref=halo_g, send_sem=halo_send.at[2 * blocks], recv_sem=halo_recv.at[2 * blocks],
         device_id={"gx": lower}, device_id_type=MESH)
 
+    halo_first = pltpu.make_async_remote_copy(
+        src_ref=grad.at[0, 0], dst_ref=halo_own, send_sem=halo_send.at[2 * blocks + 1], recv_sem=halo_recv.at[2 * blocks + 1],
+        device_id={"gx": lower}, device_id_type=MESH)
+
+    def written(d, l):
+        return pltpu.make_async_copy(grad.at[d, l], out_hbm.at[d, l], out_sem.at[d, l])
+
     def returned(c):
         rows = pl.ds(c * ROWS, ROWS)
         return pltpu.make_async_remote_copy(
@@ -89,8 +96,9 @@
 
     @pl.when(me > 0)
     def _():
-        for copy in halo_pa(0):
-            copy.start()
+        for c in range(blocks // 2):
+            for copy in halo_pa(c):
+                copy.start()
 
     for copy in first[3:]:
         copy.start()
@@ -108,9 +116,6 @@
     @pl.when(me > 0)
     def _():
         halo_k.start()
-        for c in range(1, blocks):
-            for copy in halo_pa(c):
-                copy.start()
 
     for copy in first[2:]:
         copy.wait()
@@ -124,6 +129,13 @@
         def _():
             for copy in loads(l + 1):
                 copy.wait()
+
+        @pl.when(jnp.logical_and(l == 1, me > 0))
+        def _():
+            halo_first.start()
+            for c in range(blocks // 2, blocks):
+                for copy in halo_pa(c):
+                    copy.start()
 
         def block(b, total):
             r = pl.multiple_of(b * ROWS, ROWS)
@@ -166,14 +178,23 @@
             grad[0, l + 1, here] = w * k0
             return total + jnp.where(l > 0, 1.0, 0.0) * fold(log0)
 
-        return lax.cond(l < last, lambda total: lax.fori_loop(0, blocks, cross, total), lambda total: total, total)
+        written(1, l).start()
+        written(2, l).start()
+        total = lax.cond(l < last, lambda total: lax.fori_loop(0, blocks, cross, total), lambda total: total, total)
+
+        @pl.when(jnp.logical_and(l > 0, l < last))
+        def _():
+            written(0, l).start()
+
+        return total
 
     total = lax.fori_loop(0, layers, layer, jnp.zeros((8, width), jnp.float32))
-    part[...] = total
+    part[...] = total + jnp.where(me == 0, 1.0, 0.0) * fold(grad[0, 0])
 
     @pl.when(me < n - 1)
     def _():
         halo_k.wait_recv()
+        halo_first.wait_recv()
         for c in range(blocks):
             for copy in halo_pa(c):
                 copy.wait_recv()
@@ -184,35 +205,39 @@
             k0, g_up = k[0, last, here], halo_g[here]
             factor = multiplier(code[0, last, here]) * act[last, here].astype(jnp.float32)
             w = weight(prod, factor, k0, g_up)
-            ret_out[here] = w * k0
+            w_up = w * k0
+            ret_out[here] = w_up
             returned(c).start()
             grad[0, last, here] = grad[0, last, here] + w * g_up
+            part[...] = part[...] + fold(halo_own[here] + w_up)
 
     part[...] = part[...] + fold(grad[0, last])
 
+    def to_peer(j):
+        return pltpu.make_async_remote_copy(
+            src_ref=part, dst_ref=parts.at[j - 1], send_sem=part_send.at[j - 1], recv_sem=part_recv.at[j - 1],
+            device_id={"gx": lax.rem(me + j, n)}, device_id_type=MESH)
+
+    def send(j, carry):
+        to_peer(j).start()
+        return carry
+
+    def receive(j, carry):
+        to_peer(j).wait_recv()
+        return carry
+
+    lax.fori_loop(1, n, send, 0)
+    written(0, last).start()
+
     @pl.when(me > 0)
     def _():
+        halo_first.wait_send()
         for c in range(blocks):
             here = pl.ds(c * ROWS, ROWS)
             returned(c).wait_recv()
             grad[0, 0, here] = grad[0, 0, here] + ret_in[here]
 
-    part[...] = part[...] + fold(grad[0, 0])
-
-    def to_peer(j):
-        return pltpu.make_async_remote_copy(
-            src_ref=part, dst_ref=parts.at[j - 1], send_sem=part_send.at[j - 1], recv_sem=part_recv.at[j - 1],
-            device_id={"gx": lax.rem(me + j, n)}, device_id_type=MESH)
-
-    def send(j, carry):
-        to_peer(j).start()
-        return carry
-
-    def receive(j, carry):
-        to_peer(j).wait_recv()
-        return carry
-
-    lax.fori_loop(1, n, send, 0)
+    written(0, 0).start()
     lax.fori_loop(1, n, receive, 0)
     whole = jnp.sum(jnp.sum(parts[...], axis=0) + part[...], keepdims=True)
     scale[...] = jnp.broadcast_to(lax.rsqrt(whole / entries + epsilon), scale.shape)
@@ -234,6 +259,13 @@
     def _():
         for c in range(blocks):
             returned(c).wait_send()
+
+    def finish(l, carry):
+        for d in range(3):
+            written(d, l).wait()
+        return carry
+
+    lax.fori_loop(0, layers, finish, 0)
 
 
 def local(pressure, adjoint, permeability, active, fault_codes):
@@ -248,18 +280,20 @@
         functools.partial(kernel, n, entries),
         out_shape=(
             jax.ShapeDtypeStruct((3, layers, height, width), f32),
-            jax.ShapeDtypeStruct((8, width), f32),
+            jax.ShapeDtypeStruct((height, width), f32),
         ),
         in_specs=[pl.BlockSpec(memory_space=pltpu.HBM)] * 5,
-        out_specs=(pl.BlockSpec(memory_space=pltpu.VMEM), pl.BlockSpec(memory_space=pltpu.VMEM)),
+        out_specs=(pl.BlockSpec(memory_space=pltpu.HBM), pl.BlockSpec(memory_space=pltpu.VMEM)),
         scratch_shapes=[
             pltpu.VMEM((steps, layers, padded, width), f32),
             pltpu.VMEM((steps, layers, padded, width), f32),
             pltpu.VMEM((3, layers, padded, width), f32),
             pltpu.VMEM((layers, padded, width), jnp.int32),
             pltpu.VMEM((3, layers, height, width), jnp.int32),
+            pltpu.VMEM((3, layers, height, width), f32),
             pltpu.VMEM((steps, height, width), f32),
             pltpu.VMEM((steps, height, width), f32),
+            pltpu.VMEM((height, width), f32),
             pltpu.VMEM((height, width), f32),
             pltpu.VMEM((height, width), f32),
             pltpu.VMEM((height, width), f32),
@@ -268,17 +302,18 @@
             pltpu.VMEM((8, width), f32),
             pltpu.VMEM((n - 1, 8, width), f32),
             dma((5, layers)),
-            dma((2 * blocks + 1,)),
-            dma((2 * blocks + 1,)),
+            dma((3, layers)),
+            dma((2 * blocks + 2,)),
+            dma((2 * blocks + 2,)),
             dma((blocks,)),
             dma((blocks,)),
             dma((n - 1,)),
             dma((n - 1,)),
         ],
-        compiler_params=pltpu.CompilerParams(collective_id=0, has_side_effects=True, vmem_limit_bytes=40 * 1024 * 1024),
+        compiler_params=pltpu.CompilerParams(collective_id=0, has_side_effects=True, vmem_limit_bytes=60 * 1024 * 1024),
         cost_estimate=pl.CostEstimate(flops=100_000_000, bytes_accessed=12_000_000, transcendentals=0),
     )(pressure, adjoint, permeability, active, fault_codes)
-    return grad * scale[0, 0]
+    return grad * scale
 
 
 def solution(mesh):

time: 36.4 us -> 27.3 us (0.75)
  local copies, waits for them, and re-layouts: 8.44 us -> 0 us
  Pallas kernels: 25.8 us -> 24.4 us
  other arithmetic: 1.86 us -> 2.72 us
    unnamed x10 -> x0, local copies, waits for them, and re-layouts: 7.93 us -> none
    pallas_call x1, Pallas kernels: 25.8 us -> 24.4 us  [local(): pl.pallas_call(functools.partial(kernel, n, entries), out_shape=(jax.Shap...]
    mul x1, other arithmetic: 1.86 us -> 2.72 us  [local(): return grad * scale]
    slice x1 -> x0, local copies, waits for them, and re-layouts: 0.51 us -> none  [local(): return grad * scale[0, 0]]
where the time goes in v2:
time: 27.3 us; the launch traced here: 27.2 us
  Pallas kernels  24.4 us (89%)
  other arithmetic  2.72 us (10%)
    pallas_call x1, Pallas kernels, local(): pl.pallas_call(functools.partial(kernel, n, entries), out_shape=(jax.Shap...  24.4 us
    mul x1, other arithmetic, local(): return grad * scale  2.72 us

profile of v2, /device:TPU:0, one launch (start us, length us, event | category | flops | bytes accessed | tf_op | source)
XLA Modules:
  0.0 27.2 jit_solution(15185033127470053164)
XLA Ops:
  0.0 24.4 %shard_map.55 = (f32[3,8,128,128]{3,2,1,0:T(8,128)}, f32[128,128]{1,0:T(8,128)}) custom-call(f32[7,8,128,128]{3,2,1,0:T(8,128)} %p_hbm.1, f32[7,8,128,128]{3,2,1,0:T(8,128)} %a_hbm.1, f32[3,8,128,128]{3,2,1,0:T(8,128)} %k_hbm.1, s32[8,128,128]{2,1,0:T(8,128)} %act_hbm.1, s32[3,8,128,128]{3,2,1,0:T(8,128)} %code_hbm.1), custom_call_target="tpu_custom_call" | custom-call | flops 100000000 | bytes 12000000 | tf_op jit(solution)/shard_map/pallas_call | solution.py:279
  24.4 2.7 %broadcast_multiply_fusion = f32[3,8,128,128]{3,2,1,0:T(8,128)} fusion(f32[3,8,128,128]{3,2,1,0:T(8,128)} %get-tuple-element.7, f32[128,128]{1,0:T(8,128)} %get-tuple-element.8), kind=kLoop, calls=%fused_computation | loop fusion | flops 393216 | bytes 3211264 | tf_op jit(solution)/shard_map/mul | solution.py:316

commit v3 on v2

--- a/solution.py
+++ b/solution.py
@@ -11,6 +11,7 @@
 epsilon = 1e-06
 ROWS = 32
 PAD = 8
+GRANT = 58_000_000
 
 
 def multiplier(codes):
@@ -30,10 +31,18 @@
     return 2.0 * factor * products * (k_lo * k_up) / (summed * summed)
 
 
+def distances(n):
+    reach, rounds = 1, []
+    while reach < n - 1:
+        rounds.append(reach)
+        reach *= 2
+    return rounds
+
+
 def kernel(
-    n, entries, p_hbm, a_hbm, k_hbm, act_hbm, code_hbm, out_hbm, scale,
-    p, a, k, act, code, grad, halo_p, halo_a, halo_g, halo_own, g_out, ret_out, ret_in, tail, part, parts,
-    load_sem, out_sem, halo_send, halo_recv, ret_send, ret_recv, part_send, part_recv,
+    n, entries, p_hbm, a_hbm, k_hbm, act_hbm, code_hbm, grad,
+    p, a, k, act, code, halo_p, halo_a, halo_g, halo_own, g_out, ret_out, ret_in, tail, part, parts,
+    load_sem, halo_send, halo_recv, ret_send, ret_recv, part_send, part_recv, near_sem,
 ):
     me = lax.axis_index("gx")
     lower, upper = me - 1, me + 1
@@ -43,11 +52,17 @@
 
     barrier = pltpu.get_barrier_semaphore()
 
-    def greet(j, carry):
-        pl.semaphore_signal(barrier, inc=1, device_id={"gx": lax.rem(me + j, n)}, device_id_type=MESH)
-        return carry
-
-    lax.fori_loop(1, n, greet, 0)
+    def signal(semaphore, distance):
+        for there, inside in ((me - distance, me >= distance), (me + distance, me + distance < n)):
+            @pl.when(inside)
+            def _():
+                pl.semaphore_signal(semaphore, inc=1, device_id={"gx": there}, device_id_type=MESH)
+
+    def await_signals(semaphore, distance):
+        peers = jnp.where(me >= distance, 1, 0) + jnp.where(me + distance < n, 1, 0)
+        pl.semaphore_wait(semaphore, peers)
+
+    signal(barrier, 1)
 
     def loads(l):
         return (
@@ -79,9 +94,6 @@
         src_ref=grad.at[0, 0], dst_ref=halo_own, send_sem=halo_send.at[2 * blocks + 1], recv_sem=halo_recv.at[2 * blocks + 1],
         device_id={"gx": lower}, device_id_type=MESH)
 
-    def written(d, l):
-        return pltpu.make_async_copy(grad.at[d, l], out_hbm.at[d, l], out_sem.at[d, l])
-
     def returned(c):
         rows = pl.ds(c * ROWS, ROWS)
         return pltpu.make_async_remote_copy(
@@ -92,7 +104,7 @@
     for copy in first[:3]:
         copy.start()
 
-    pl.semaphore_wait(barrier, n - 1)
+    await_signals(barrier, 1)
 
     @pl.when(me > 0)
     def _():
@@ -178,17 +190,13 @@
             grad[0, l + 1, here] = w * k0
             return total + jnp.where(l > 0, 1.0, 0.0) * fold(log0)
 
-        written(1, l).start()
-        written(2, l).start()
-        total = lax.cond(l < last, lambda total: lax.fori_loop(0, blocks, cross, total), lambda total: total, total)
-
-        @pl.when(jnp.logical_and(l > 0, l < last))
-        def _():
-            written(0, l).start()
-
-        return total
+        return lax.cond(l < last, lambda total: lax.fori_loop(0, blocks, cross, total), lambda total: total, total)
 
     total = lax.fori_loop(0, layers, layer, jnp.zeros((8, width), jnp.float32))
+    for i, distance in enumerate(distances(n)):
+        signal(near_sem.at[i], distance)
+        await_signals(near_sem.at[i], distance)
+
     part[...] = total + jnp.where(me == 0, 1.0, 0.0) * fold(grad[0, 0])
 
     @pl.when(me < n - 1)
@@ -207,7 +215,6 @@
             w = weight(prod, factor, k0, g_up)
             w_up = w * k0
             ret_out[here] = w_up
-            returned(c).start()
             grad[0, last, here] = grad[0, last, here] + w * g_up
             part[...] = part[...] + fold(halo_own[here] + w_up)
 
@@ -227,7 +234,11 @@
         return carry
 
     lax.fori_loop(1, n, send, 0)
-    written(0, last).start()
+
+    @pl.when(me < n - 1)
+    def _():
+        for c in range(blocks):
+            returned(c).start()
 
     @pl.when(me > 0)
     def _():
@@ -237,10 +248,18 @@
             returned(c).wait_recv()
             grad[0, 0, here] = grad[0, 0, here] + ret_in[here]
 
-    written(0, 0).start()
     lax.fori_loop(1, n, receive, 0)
     whole = jnp.sum(jnp.sum(parts[...], axis=0) + part[...], keepdims=True)
-    scale[...] = jnp.broadcast_to(lax.rsqrt(whole / entries + epsilon), scale.shape)
+    scale = jnp.broadcast_to(lax.rsqrt(whole / entries + epsilon), (ROWS, width))
+
+    def normalize(i, carry):
+        here = pl.ds(pl.multiple_of(i * ROWS, ROWS), ROWS)
+        for d in range(3):
+            for l in range(layers):
+                grad[d, l, here] = grad[d, l, here] * scale
+        return carry
+
+    lax.fori_loop(0, blocks, normalize, 0)
 
     def drain(j, carry):
         to_peer(j).wait_send()
@@ -259,13 +278,6 @@
     def _():
         for c in range(blocks):
             returned(c).wait_send()
-
-    def finish(l, carry):
-        for d in range(3):
-            written(d, l).wait()
-        return carry
-
-    lax.fori_loop(0, layers, finish, 0)
 
 
 def local(pressure, adjoint, permeability, active, fault_codes):
@@ -276,21 +288,17 @@
     f32 = jnp.float32
     padded = height + PAD
     dma = pltpu.SemaphoreType.DMA
-    grad, scale = pl.pallas_call(
+    return pl.pallas_call(
         functools.partial(kernel, n, entries),
-        out_shape=(
-            jax.ShapeDtypeStruct((3, layers, height, width), f32),
-            jax.ShapeDtypeStruct((height, width), f32),
-        ),
+        out_shape=pltpu.VMEM((3, layers, height, width), f32),
         in_specs=[pl.BlockSpec(memory_space=pltpu.HBM)] * 5,
-        out_specs=(pl.BlockSpec(memory_space=pltpu.HBM), pl.BlockSpec(memory_space=pltpu.VMEM)),
+        out_specs=pl.BlockSpec(memory_space=pltpu.VMEM),
         scratch_shapes=[
             pltpu.VMEM((steps, layers, padded, width), f32),
             pltpu.VMEM((steps, layers, padded, width), f32),
             pltpu.VMEM((3, layers, padded, width), f32),
             pltpu.VMEM((layers, padded, width), jnp.int32),
             pltpu.VMEM((3, layers, height, width), jnp.int32),
-            pltpu.VMEM((3, layers, height, width), f32),
             pltpu.VMEM((steps, height, width), f32),
             pltpu.VMEM((steps, height, width), f32),
             pltpu.VMEM((height, width), f32),
@@ -302,18 +310,17 @@
             pltpu.VMEM((8, width), f32),
             pltpu.VMEM((n - 1, 8, width), f32),
             dma((5, layers)),
-            dma((3, layers)),
             dma((2 * blocks + 2,)),
             dma((2 * blocks + 2,)),
             dma((blocks,)),
             dma((blocks,)),
             dma((n - 1,)),
             dma((n - 1,)),
+            pltpu.SemaphoreType.REGULAR((len(distances(n)),)),
         ],
-        compiler_params=pltpu.CompilerParams(collective_id=0, has_side_effects=True, vmem_limit_bytes=60 * 1024 * 1024),
+        compiler_params=pltpu.CompilerParams(collective_id=0, has_side_effects=True, vmem_limit_bytes=GRANT),
         cost_estimate=pl.CostEstimate(flops=100_000_000, bytes_accessed=12_000_000, transcendentals=0),
     )(pressure, adjoint, permeability, active, fault_codes)
-    return grad * scale
 
 
 def solution(mesh):

time: 27.3 us -> 26.7 us (0.978)
  other arithmetic: 2.72 us -> 0 us
  local copies, waits for them, and re-layouts: 0 us -> 1.15 us
  Pallas kernels: 24.4 us -> 25.4 us
    mul x1 -> x0, other arithmetic: 2.72 us -> none  [local(): return grad * scale]
    unnamed x0 -> x1, local copies, waits for them, and re-layouts: none -> 1.15 us
    pallas_call x1, Pallas kernels: 24.4 us -> 25.4 us  [local(): pl.pallas_call(functools.partial(kernel, n, entries), out_shape=pltpu.VME...]
where the time goes in v3:
time: 26.7 us; the launch traced here: 26.6 us
  Pallas kernels  25.4 us (95%)
  local copies, waits for them, and re-layouts  1.15 us (4%)
    pallas_call x1, Pallas kernels, local(): pl.pallas_call(functools.partial(kernel, n, entries), out_shape=pltpu.VME...  25.4 us
    unnamed x1, local copies, waits for them, and re-layouts  1.15 us

profile of v3, /device:TPU:0, one launch (start us, length us, event | category | flops | bytes accessed | tf_op | source)
XLA Modules:
  0.0 26.6 jit_solution(16182039375065075974)
XLA Ops:
  0.0 25.4 %shard_map.55 = f32[3,8,128,128]{3,2,1,0:T(8,128)S(1)} custom-call(f32[7,8,128,128]{3,2,1,0:T(8,128)} %p_hbm.1, f32[7,8,128,128]{3,2,1,0:T(8,128)} %a_hbm.1, f32[3,8,128,128]{3,2,1,0:T(8,128)} %k_hbm.1, s32[8,128,128]{2,1,0:T(8,128)} %act_hbm.1, s32[3,8,128,128]{3,2,1,0:T(8,128)} %code_hbm.1), custom_call_target="tpu_custom_call" | custom-call | flops 100000000 | bytes 12000000 | tf_op jit(solution)/shard_map/pallas_call | solution.py:291
  25.4 1.1 %copy.7 = f32[3,8,128,128]{3,2,1,0:T(8,128)} copy(f32[3,8,128,128]{3,2,1,0:T(8,128)S(1)} %shard_map.55) | data formatting | bytes 3145728

commit v4 on v3

--- a/solution.py
+++ b/solution.py
@@ -41,7 +41,7 @@
 
 def kernel(
     n, entries, p_hbm, a_hbm, k_hbm, act_hbm, code_hbm, grad,
-    p, a, k, act, code, halo_p, halo_a, halo_g, halo_own, g_out, ret_out, ret_in, tail, part, parts,
+    p, a, k, act, code, halo_p, halo_a, halo_g, halo_own, g_out, ret_out, ret_in, tail, acc, part, parts,
     load_sem, halo_send, halo_recv, ret_send, ret_recv, part_send, part_recv, near_sem,
 ):
     me = lax.axis_index("gx")
@@ -91,7 +91,7 @@
         device_id={"gx": lower}, device_id_type=MESH)
 
     halo_first = pltpu.make_async_remote_copy(
-        src_ref=grad.at[0, 0], dst_ref=halo_own, send_sem=halo_send.at[2 * blocks + 1], recv_sem=halo_recv.at[2 * blocks + 1],
+        src_ref=grad.at[0, 0, pl.ds(height - ROWS, ROWS)], dst_ref=halo_own, send_sem=halo_send.at[2 * blocks + 1], recv_sem=halo_recv.at[2 * blocks + 1],
         device_id={"gx": lower}, device_id_type=MESH)
 
     def returned(c):
@@ -197,12 +197,11 @@
         signal(near_sem.at[i], distance)
         await_signals(near_sem.at[i], distance)
 
-    part[...] = total + jnp.where(me == 0, 1.0, 0.0) * fold(grad[0, 0])
+    acc[...] = total + jnp.where(me == 0, 1.0, 0.0) * fold(grad[0, 0])
 
     @pl.when(me < n - 1)
     def _():
         halo_k.wait_recv()
-        halo_first.wait_recv()
         for c in range(blocks):
             for copy in halo_pa(c):
                 copy.wait_recv()
@@ -216,9 +215,27 @@
             w_up = w * k0
             ret_out[here] = w_up
             grad[0, last, here] = grad[0, last, here] + w * g_up
-            part[...] = part[...] + fold(halo_own[here] + w_up)
-
-    part[...] = part[...] + fold(grad[0, last])
+            if c < blocks - 1:
+                returned(c).start()
+            else:
+                halo_first.wait_recv()
+                acc[...] = acc[...] + fold(halo_own[...] + w_up)
+
+    def take_back(c):
+        here = pl.ds(c * ROWS, ROWS)
+        returned(c).wait_recv()
+        log0 = grad[0, 0, here] + ret_in[here]
+        grad[0, 0, here] = log0
+        return fold(log0)
+
+    @pl.when(me > 0)
+    def _():
+        halo_first.wait_send()
+        for c in range(blocks - 1):
+            acc[...] = acc[...] + take_back(c)
+
+    mine = jnp.sum(acc[...] + fold(grad[0, last]), axis=0, keepdims=True)
+    part[...] = mine
 
     def to_peer(j):
         return pltpu.make_async_remote_copy(
@@ -237,19 +254,14 @@
 
     @pl.when(me < n - 1)
     def _():
-        for c in range(blocks):
-            returned(c).start()
-
-    @pl.when(me > 0)
-    def _():
-        halo_first.wait_send()
-        for c in range(blocks):
-            here = pl.ds(c * ROWS, ROWS)
-            returned(c).wait_recv()
-            grad[0, 0, here] = grad[0, 0, here] + ret_in[here]
+        returned(blocks - 1).start()
+
+    @pl.when(me > 0)
+    def _():
+        take_back(blocks - 1)
 
     lax.fori_loop(1, n, receive, 0)
-    whole = jnp.sum(jnp.sum(parts[...], axis=0) + part[...], keepdims=True)
+    whole = jnp.sum(jnp.sum(parts[...], axis=0) + mine, keepdims=True)
     scale = jnp.broadcast_to(lax.rsqrt(whole / entries + epsilon), (ROWS, width))
 
     def normalize(i, carry):
@@ -302,13 +314,14 @@
             pltpu.VMEM((steps, height, width), f32),
             pltpu.VMEM((steps, height, width), f32),
             pltpu.VMEM((height, width), f32),
-            pltpu.VMEM((height, width), f32),
+            pltpu.VMEM((ROWS, width), f32),
             pltpu.VMEM((height, width), f32),
             pltpu.VMEM((height, width), f32),
             pltpu.VMEM((height, width), f32),
             pltpu.VMEM((padded, width), f32),
             pltpu.VMEM((8, width), f32),
-            pltpu.VMEM((n - 1, 8, width), f32),
+            pltpu.VMEM((1, width), f32),
+            pltpu.VMEM((n - 1, 1, width), f32),
             dma((5, layers)),
             dma((2 * blocks + 2,)),
             dma((2 * blocks + 2,)),

time: 26.7 us -> 27.5 us (1.030)
  Pallas kernels: 25.4 us -> 26.2 us
    pallas_call x1, Pallas kernels: 25.4 us -> 26.2 us  [local(): pl.pallas_call(functools.partial(kernel, n, entries), out_shape=pltpu.VME...]
where the time goes in v4:
time: 27.5 us; the launch traced here: 27.3 us
  Pallas kernels  26.2 us (95%)
  local copies, waits for them, and re-layouts  1.15 us (4%)
    pallas_call x1, Pallas kernels, local(): pl.pallas_call(functools.partial(kernel, n, entries), out_shape=pltpu.VME...  26.2 us
    unnamed x1, local copies, waits for them, and re-layouts  1.15 us

profile of v4, /device:TPU:0, one launch (start us, length us, event | category | flops | bytes accessed | tf_op | source)
XLA Modules:
  0.0 27.3 jit_solution(9501566381574475797)
XLA Ops:
  0.0 26.2 %shard_map.55 = f32[3,8,128,128]{3,2,1,0:T(8,128)S(1)} custom-call(f32[7,8,128,128]{3,2,1,0:T(8,128)} %p_hbm.1, f32[7,8,128,128]{3,2,1,0:T(8,128)} %a_hbm.1, f32[3,8,128,128]{3,2,1,0:T(8,128)} %k_hbm.1, s32[8,128,128]{2,1,0:T(8,128)} %act_hbm.1, s32[3,8,128,128]{3,2,1,0:T(8,128)} %code_hbm.1), custom_call_target="tpu_custom_call" | custom-call | flops 100000000 | bytes 12000000 | tf_op jit(solution)/shard_map/pallas_call | solution.py:303
  26.2 1.1 %copy.7 = f32[3,8,128,128]{3,2,1,0:T(8,128)} copy(f32[3,8,128,128]{3,2,1,0:T(8,128)S(1)} %shard_map.55) | data formatting | bytes 3145728

commit v5 on v4

--- a/solution.py
+++ b/solution.py
@@ -31,18 +31,10 @@
     return 2.0 * factor * products * (k_lo * k_up) / (summed * summed)
 
 
-def distances(n):
-    reach, rounds = 1, []
-    while reach < n - 1:
-        rounds.append(reach)
-        reach *= 2
-    return rounds
-
-
 def kernel(
     n, entries, p_hbm, a_hbm, k_hbm, act_hbm, code_hbm, grad,
     p, a, k, act, code, halo_p, halo_a, halo_g, halo_own, g_out, ret_out, ret_in, tail, acc, part, parts,
-    load_sem, halo_send, halo_recv, ret_send, ret_recv, part_send, part_recv, near_sem,
+    load_sem, halo_send, halo_recv, ret_send, ret_recv, part_send, part_recv,
 ):
     me = lax.axis_index("gx")
     lower, upper = me - 1, me + 1
@@ -52,17 +44,11 @@
 
     barrier = pltpu.get_barrier_semaphore()
 
-    def signal(semaphore, distance):
-        for there, inside in ((me - distance, me >= distance), (me + distance, me + distance < n)):
-            @pl.when(inside)
-            def _():
-                pl.semaphore_signal(semaphore, inc=1, device_id={"gx": there}, device_id_type=MESH)
-
-    def await_signals(semaphore, distance):
-        peers = jnp.where(me >= distance, 1, 0) + jnp.where(me + distance < n, 1, 0)
-        pl.semaphore_wait(semaphore, peers)
-
-    signal(barrier, 1)
+    def greet(j, carry):
+        pl.semaphore_signal(barrier, inc=1, device_id={"gx": lax.rem(me + j, n)}, device_id_type=MESH)
+        return carry
+
+    lax.fori_loop(1, n, greet, 0)
 
     def loads(l):
         return (
@@ -104,7 +90,7 @@
     for copy in first[:3]:
         copy.start()
 
-    await_signals(barrier, 1)
+    pl.semaphore_wait(barrier, n - 1)
 
     @pl.when(me > 0)
     def _():
@@ -193,10 +179,6 @@
         return lax.cond(l < last, lambda total: lax.fori_loop(0, blocks, cross, total), lambda total: total, total)
 
     total = lax.fori_loop(0, layers, layer, jnp.zeros((8, width), jnp.float32))
-    for i, distance in enumerate(distances(n)):
-        signal(near_sem.at[i], distance)
-        await_signals(near_sem.at[i], distance)
-
     acc[...] = total + jnp.where(me == 0, 1.0, 0.0) * fold(grad[0, 0])
 
     @pl.when(me < n - 1)
@@ -329,7 +311,6 @@
             dma((blocks,)),
             dma((n - 1,)),
             dma((n - 1,)),
-            pltpu.SemaphoreType.REGULAR((len(distances(n)),)),
         ],
         compiler_params=pltpu.CompilerParams(collective_id=0, has_side_effects=True, vmem_limit_bytes=GRANT),
         cost_estimate=pl.CostEstimate(flops=100_000_000, bytes_accessed=12_000_000, transcendentals=0),

time: 27.5 us -> 25.3 us (0.920)
  Pallas kernels: 26.2 us -> 24 us
    pallas_call x1, Pallas kernels: 26.2 us -> 24 us  [local(): pl.pallas_call(functools.partial(kernel, n, entries), out_shape=pltpu.VME...]
where the time goes in v5:
time: 25.3 us; the launch traced here: 25.2 us
  Pallas kernels  24 us (95%)
  local copies, waits for them, and re-layouts  1.15 us (5%)
    pallas_call x1, Pallas kernels, local(): pl.pallas_call(functools.partial(kernel, n, entries), out_shape=pltpu.VME...  24 us
    unnamed x1, local copies, waits for them, and re-layouts  1.15 us

profile of v5, /device:TPU:0, one launch (start us, length us, event | category | flops | bytes accessed | tf_op | source)
XLA Modules:
  0.0 25.2 jit_solution(4089280422189322761)
XLA Ops:
  0.0 24.0 %shard_map.55 = f32[3,8,128,128]{3,2,1,0:T(8,128)S(1)} custom-call(f32[7,8,128,128]{3,2,1,0:T(8,128)} %p_hbm.1, f32[7,8,128,128]{3,2,1,0:T(8,128)} %a_hbm.1, f32[3,8,128,128]{3,2,1,0:T(8,128)} %k_hbm.1, s32[8,128,128]{2,1,0:T(8,128)} %act_hbm.1, s32[3,8,128,128]{3,2,1,0:T(8,128)} %code_hbm.1), custom_call_target="tpu_custom_call" | custom-call | flops 100000000 | bytes 12000000 | tf_op jit(solution)/shard_map/pallas_call | solution.py:285
  24.0 1.1 %copy.7 = f32[3,8,128,128]{3,2,1,0:T(8,128)} copy(f32[3,8,128,128]{3,2,1,0:T(8,128)S(1)} %shard_map.55) | data formatting | bytes 3145728

commit v6 on v4

--- a/solution.py
+++ b/solution.py
@@ -63,6 +63,13 @@
         pl.semaphore_wait(semaphore, peers)
 
     signal(barrier, 1)
+    rounds = distances(n)
+
+    def turn(i):
+        if i > 0:
+            await_signals(near_sem.at[i - 1], rounds[i - 1])
+        if i < len(rounds):
+            signal(near_sem.at[i], rounds[i])
 
     def loads(l):
         return (
@@ -105,6 +112,7 @@
         copy.start()
 
     await_signals(barrier, 1)
+    turn(0)
 
     @pl.when(me > 0)
     def _():
@@ -148,6 +156,11 @@
             for c in range(blocks // 2, blocks):
                 for copy in halo_pa(c):
                     copy.start()
+
+        for i in range(1, min(layers - 1, len(rounds) + 1)):
+            @pl.when(l == i + 1)
+            def _(i=i):
+                turn(i)
 
         def block(b, total):
             r = pl.multiple_of(b * ROWS, ROWS)
@@ -193,9 +206,8 @@
         return lax.cond(l < last, lambda total: lax.fori_loop(0, blocks, cross, total), lambda total: total, total)
 
     total = lax.fori_loop(0, layers, layer, jnp.zeros((8, width), jnp.float32))
-    for i, distance in enumerate(distances(n)):
-        signal(near_sem.at[i], distance)
-        await_signals(near_sem.at[i], distance)
+    for i in range(layers - 1, len(rounds) + 1):
+        turn(i)
 
     acc[...] = total + jnp.where(me == 0, 1.0, 0.0) * fold(grad[0, 0])
 

time: 27.5 us -> 24.6 us (0.89)
  Pallas kernels: 26.2 us -> 23.3 us
    pallas_call x1, Pallas kernels: 26.2 us -> 23.3 us  [local(): pl.pallas_call(functools.partial(kernel, n, entries), out_shape=pltpu.VME...]
where the time goes in v6:
time: 24.6 us; the launch traced here: 24.4 us
  Pallas kernels  23.3 us (95%)
  local copies, waits for them, and re-layouts  1.15 us (5%)
    pallas_call x1, Pallas kernels, local(): pl.pallas_call(functools.partial(kernel, n, entries), out_shape=pltpu.VME...  23.3 us
    unnamed x1, local copies, waits for them, and re-layouts  1.15 us

profile of v6, /device:TPU:0, one launch (start us, length us, event | category | flops | bytes accessed | tf_op | source)
XLA Modules:
  0.0 24.4 jit_solution(3917458930546622582)
XLA Ops:
  0.0 23.3 %shard_map.55 = f32[3,8,128,128]{3,2,1,0:T(8,128)S(1)} custom-call(f32[7,8,128,128]{3,2,1,0:T(8,128)} %p_hbm.1, f32[7,8,128,128]{3,2,1,0:T(8,128)} %a_hbm.1, f32[3,8,128,128]{3,2,1,0:T(8,128)} %k_hbm.1, s32[8,128,128]{2,1,0:T(8,128)} %act_hbm.1, s32[3,8,128,128]{3,2,1,0:T(8,128)} %code_hbm.1), custom_call_target="tpu_custom_call" | custom-call | flops 100000000 | bytes 12000000 | tf_op jit(solution)/shard_map/pallas_call | solution.py:315
  23.3 1.1 %copy.7 = f32[3,8,128,128]{3,2,1,0:T(8,128)} copy(f32[3,8,128,128]{3,2,1,0:T(8,128)S(1)} %shard_map.55) | data formatting | bytes 3145728

commit v7 on v6

--- a/solution.py
+++ b/solution.py
@@ -62,12 +62,20 @@
         peers = jnp.where(me >= distance, 1, 0) + jnp.where(me + distance < n, 1, 0)
         pl.semaphore_wait(semaphore, peers)
 
-    signal(barrier, 1)
+    @pl.when(upper < n)
+    def _():
+        pl.semaphore_signal(barrier, inc=1, device_id={"gx": upper}, device_id_type=MESH)
+
     rounds = distances(n)
 
     def turn(i):
         if i > 0:
             await_signals(near_sem.at[i - 1], rounds[i - 1])
+        else:
+            @pl.when(upper < n)
+            def _():
+                pl.semaphore_wait(near_sem.at[len(rounds)], 1)
+
         if i < len(rounds):
             signal(near_sem.at[i], rounds[i])
 
@@ -111,8 +119,11 @@
     for copy in first[:3]:
         copy.start()
 
-    await_signals(barrier, 1)
-    turn(0)
+    @pl.when(me > 0)
+    def _():
+        pl.semaphore_wait(barrier, 1)
+        pl.semaphore_signal(near_sem.at[len(rounds)], inc=1, device_id={"gx": lower}, device_id_type=MESH)
+
 
     @pl.when(me > 0)
     def _():
@@ -157,7 +168,7 @@
                 for copy in halo_pa(c):
                     copy.start()
 
-        for i in range(1, min(layers - 1, len(rounds) + 1)):
+        for i in range(0, min(layers - 1, len(rounds) + 1)):
             @pl.when(l == i + 1)
             def _(i=i):
                 turn(i)
@@ -341,7 +352,7 @@
             dma((blocks,)),
             dma((n - 1,)),
             dma((n - 1,)),
-            pltpu.SemaphoreType.REGULAR((len(distances(n)),)),
+            pltpu.SemaphoreType.REGULAR((len(distances(n)) + 1,)),
         ],
         compiler_params=pltpu.CompilerParams(collective_id=0, has_side_effects=True, vmem_limit_bytes=GRANT),
         cost_estimate=pl.CostEstimate(flops=100_000_000, bytes_accessed=12_000_000, transcendentals=0),

time: 24.6 us -> 24.6 us (level)
  no operation moved by 1% of the time
where the time goes in v7:
time: 24.6 us; the launch traced here: 24.4 us
  Pallas kernels  23.3 us (95%)
  local copies, waits for them, and re-layouts  1.15 us (5%)
    pallas_call x1, Pallas kernels, local(): pl.pallas_call(functools.partial(kernel, n, entries), out_shape=pltpu.VME...  23.3 us
    unnamed x1, local copies, waits for them, and re-layouts  1.15 us

profile of v7, /device:TPU:0, one launch (start us, length us, event | category | flops | bytes accessed | tf_op | source)
XLA Modules:
  0.0 24.4 jit_solution(8520292069927473896)
XLA Ops:
  0.0 23.3 %shard_map.55 = f32[3,8,128,128]{3,2,1,0:T(8,128)S(1)} custom-call(f32[7,8,128,128]{3,2,1,0:T(8,128)} %p_hbm.1, f32[7,8,128,128]{3,2,1,0:T(8,128)} %a_hbm.1, f32[3,8,128,128]{3,2,1,0:T(8,128)} %k_hbm.1, s32[8,128,128]{2,1,0:T(8,128)} %act_hbm.1, s32[3,8,128,128]{3,2,1,0:T(8,128)} %code_hbm.1), custom_call_target="tpu_custom_call" | custom-call | flops 100000000 | bytes 12000000 | tf_op jit(solution)/shard_map/pallas_call | solution.py:326
  23.3 1.1 %copy.7 = f32[3,8,128,128]{3,2,1,0:T(8,128)} copy(f32[3,8,128,128]{3,2,1,0:T(8,128)S(1)} %shard_map.55) | data formatting | bytes 3145728
